TPU v7x, 32 devices: a whole 2x2x4 slice. The times are simulated.
32 devices in a mesh: dp: 4 (over y, core), slab: 8 (over z, x).
Axes of the slice: x: 2, y: 2, z: 4, core: 2. Of those that a mesh axis runs over, the one named last changes fastest.
Arguments:
- acts: bfloat16 [4, 32, 8, 128, 128], P('dp', None, 'slab'), may hold values from -24 to 24
- grads: bfloat16 [4, 32, 8, 128, 128], P('dp', None, 'slab'), may hold values from -6 to 6
- picks: int32 [4, 4096], P('dp', 'slab'), may hold values from 0 to 31
Outputs:
- weight_grad: float32 [32, 864], replicated
- update: float32 [32, 864], replicated
Inputs may be any that keep to these rules, and one draw needn't show every extreme that they name: `picks`: one cell is sampled in each aligned block of 32 of a device's cells, counted plane by plane, row by row, column by column; entry e of a device's 512 entries belongs to block e.
All inputs are finite; a program needn't handle non-finite values.
Results may differ from a plain program's by a relative error of at most 0.0003.
Values may be sent and summed in bfloat16 or wider, within the bound.
A program may use at most 128 MiB of HBM per device.

v0:
```python
import math
import jax
import jax.numpy as jnp
from jax import lax
from jax.sharding import PartitionSpec as P

epsilon = 1e-06
damping = 0.1
trust_region_limit = 0.3
learning_rate = 0.01


def padded_2(shard, sides, width):
    for axis, dim in sides:
        size, length = (lax.axis_size(axis), shard.shape[dim])
        up = [(i, (i + 1) % size) for i in range(size - 1)]
        down = [(j, i) for i, j in up]
        last = lax.slice_in_dim(shard, length - width, length, axis=dim)
        leading = lax.slice_in_dim(shard, 0, width, axis=dim)
        before = lax.ppermute(last, axis, up)
        after = lax.ppermute(leading, axis, down)
        shard = jnp.concatenate([before, shard, after], axis=dim)
    return shard


def cholesky_apply(factor, values):
    halfway = lax.linalg.triangular_solve(factor, values, left_side=True, lower=True)
    return lax.linalg.triangular_solve(
        factor, halfway, left_side=True, lower=True, transpose_a=True
    )


def take_columns(matrix, indices):
    return jnp.take(matrix, indices, axis=1)


def shards(acts, grads, picks):
    volumes, channels, planes, height, kernel_extent = acts.shape
    outputs = grads.shape[1]
    sample_count = picks.shape[1]
    plane_size = (height + 2) * (kernel_extent + 2)
    shifts = jnp.array(
        [
            along_z * plane_size + along_y * (kernel_extent + 2) + along_x
            for along_z in range(3)
            for along_y in range(3)
            for along_x in range(3)
        ],
        dtype=jnp.int32,
    )
    extended = padded_2(acts, (("slab", 2),), 1)
    padded = jnp.pad(extended, ((0, 0), (0, 0), (0, 0), (1, 1), (1, 1)))
    grad_rows = grads.reshape(volumes, outputs, -1)
    products = []
    for offset in range(27):
        along_z, along_y, along_x = (offset // 9, offset // 3 % 3, offset % 3)
        shifted = padded[
            :,
            :,
            along_z : along_z + planes,
            along_y : along_y + height,
            along_x : along_x + kernel_extent,
        ].reshape(volumes, channels, -1)
        products.append(
            lax.dot_general(
                grad_rows, shifted, (((0, 2), (0, 2)), ((), ())), preferred_element_type=jnp.float32
            )
        )
    gradient_portion = jnp.concatenate(products, axis=1)
    sample_index = jnp.arange(sample_count, dtype=jnp.int32)
    position = sample_index[None, :] * 32 + picks
    plane_index = position // (height * kernel_extent)
    row_index = position // kernel_extent % height
    column_index = position % kernel_extent
    base_index = plane_index * plane_size + row_index * (kernel_extent + 2) + column_index
    flat_index = (shifts[None, :, None] + base_index[:, None, :]).reshape(volumes, -1)
    selected_values = jax.vmap(take_columns)(padded.reshape(volumes, channels, -1), flat_index)
    input_patches = selected_values.reshape(volumes, channels, 27, sample_count).transpose(
        0, 2, 1, 3
    )
    grad_samples = jax.vmap(take_columns)(grad_rows, position)
    gradient_gram_matrix = jnp.einsum(
        "vcs,vds->cd", grad_samples, grad_samples, preferred_element_type=jnp.float32
    )
    gram = jnp.einsum(
        "mfuh,mioh->fuio", input_patches, input_patches, preferred_element_type=jnp.float32
    ).reshape(27 * channels, 27 * channels)
    summed_acts, summed_grads, summed_weight = lax.psum(
        (gram, gradient_gram_matrix, gradient_portion), ("dp", "slab")
    )
    positions = (
        volumes * lax.axis_size("dp") * planes * lax.axis_size("slab") * height * kernel_extent
    )
    samples = volumes * lax.axis_size("dp") * sample_count * lax.axis_size("slab")
    weight_grad = summed_weight / math.sqrt(positions)
    factor_acts = summed_acts / samples
    factor_grads = summed_grads / samples
    patch_width = factor_acts.shape[0]
    trace_ratio = jnp.sqrt(
        (jnp.trace(factor_acts) / patch_width + epsilon)
        / (jnp.trace(factor_grads) / outputs + epsilon)
    )
    damped_activation_factor = factor_acts + trace_ratio * math.sqrt(damping) * jnp.eye(
        patch_width, dtype=jnp.float32
    )
    damped_grads = factor_grads + math.sqrt(damping) / trace_ratio * jnp.eye(
        outputs, dtype=jnp.float32
    )
    chol_acts = jnp.linalg.cholesky(damped_activation_factor)
    chol_grads = jnp.linalg.cholesky(damped_grads)
    left_solved = cholesky_apply(chol_grads, weight_grad)
    precond = cholesky_apply(chol_acts, left_solved.T).T
    quadratic = jnp.sum(precond * weight_grad)
    clip_factor = jnp.minimum(1.0, jnp.sqrt(trust_region_limit / (learning_rate**2 * quadratic)))
    return (weight_grad, clip_factor * precond)


def solution(mesh):
    return jax.shard_map(
        shards,
        mesh=mesh,
        in_specs=(
            P("dp", None, "slab", None, None),
            P("dp", None, "slab", None, None),
            P("dp", "slab"),
        ),
        out_specs=(P(), P()),
        check_vma=False,
    )
```

profile of v0, /device:TPU:0, one launch (start us, length us, event | category | flops | bytes accessed | tf_op | source)
XLA Modules:
  0.0 786.8 jit_solution(2452920314638502882)
XLA Ops:
  7.2 1.9 copy.40
  9.1 4.9 collective-permute-start
  18.2 2.8 convolution_bitcast_fusion.13
  21.0 37.8 %collective-permute-done = bf16[1,32,1,128,128]{4,1,3,2,0:T(8,128)(2,1)S(1)} collective-permute-done((bf16[1,32,1,128,128]{4,1,3,2,0:T(8,128)(2,1)S(1)}, bf16[1,32,1,128,128]{4,1,3,2,0:T(8,128)(2,1)S(1)}, u32[]{:S(2)}, u32[]{:S(2)}) %collective-permute-start) | collective-permute-done | bytes 1048608 | tf_op jit(solution)/shard_map/ppermute | solution.py:20
  58.9 7.8 select_maximum_fusion
  80.4 1.6 convolution_bitcast_fusion.24
  93.4 6.5 copy.71
  99.9 6.9 reshape.605
  106.8 8.9 %copy.72 = bf16[1,32,50700]{1,2,0:T(8,128)(2,1)} copy(bf16[1,32,50700]{2,1,0:T(8,128)(2,1)S(1)} %reshape.605) | data formatting | bytes 6489600 | tf_op jit(solution)/shard_map/reshape | solution.py:77
  115.7 209.4 %gather_fusion = bf16[13824,32]{1,0:T(8,128)(2,1)} fusion(bf16[1,32,50700]{1,2,0:T(8,128)(2,1)} %copy.72, s32[13824]{0:T(1024)S(1)} %fusion.81), kind=kCustom, calls=%fused_computation | custom fusion | bytes 1880064 | tf_op jit(solution)/shard_map/vmap(jit(_take))/gather | solution.py:34
  325.2 3.2 copy.73
  328.6 2.8 fusion.151
  334.0 3.3 copy.74
  337.4 6.0 gather_fusion.1
  343.8 41.9 %psum.23 = f32[32,32]{1,0:T(8,128)S(1)} all-reduce(f32[32,32]{1,0:T(8,128)S(1)} %fusion.34), channel_id=1, replica_groups=mesh['dp'=4,'slab'=8] {'dp','slab'}, use_global_device_ids=true, to_apply=%region_3.4 | all-reduce | flops 1024 | bytes 8192 | tf_op jit(solution)/shard_map/psum | solution.py:88
  387.6 88.0 %all-reduce.7.cloned.1.call-done = (f32[32,864]{1,0:T(8,128)}, f32[864,864]{1,0:T(8,128)}) async-done(((f32[32,864]{1,0:T(8,128)}, f32[864,864]{1,0:T(8,128)}), (f32[32,864]{1,0:T(8,128)}, f32[864,864]{1,0:T(8,128)})) %all-reduce.7.cloned.1.call-update) | async-done | bytes 3096592 | tf_op jit(solution)/shard_map/psum | solution.py:88
  475.6 2.7 select_reduce_fusion
  479.1 1.9 select_add_fusion
  481.0 4.7 copy.75
  485.7 2.3 fusion.6
  488.0 1.6 copy-done.3
  489.6 11.7 %cholesky.204 = f32[128,128]{1,0:T(8,128)S(1)} custom-call(f32[128,128]{1,0:T(8,128)S(1)} %cholesky.534), custom_call_target="Cholesky" | custom-call | tf_op jit(solution)/shard_map/jit(cholesky)/cholesky | solution.py:109
  501.6 9.8 %custom-call.64 = f32[1,128,128]{1,2,0:T(8,128)S(1)} custom-call(f32[1,128,128]{2,1,0:T(8,128)S(1)} %get-tuple-element.40), custom_call_target="InvertDiagBlocksLowerTriangular" | custom-call | tf_op jit(solution)/shard_map/jit(cholesky)/cholesky | solution.py:109
  514.9 13.2 %cholesky.227 = f32[128,128]{1,0:T(8,128)} custom-call(f32[128,128]{1,0:T(8,128)} %cholesky.538), custom_call_target="Cholesky" | custom-call | tf_op jit(solution)/shard_map/jit(cholesky)/cholesky | solution.py:109
  529.6 11.4 %custom-call.65 = f32[1,128,128]{1,2,0:T(8,128)} custom-call(f32[1,128,128]{2,1,0:T(8,128)} %get-tuple-element.37), custom_call_target="InvertDiagBlocksLowerTriangular" | custom-call | tf_op jit(solution)/shard_map/jit(cholesky)/cholesky | solution.py:109
  542.2 1.6 convolution_subtract_fusion.1
  543.9 12.3 %cholesky.432 = f32[128,128]{1,0:T(8,128)} custom-call(f32[128,128]{1,0:T(8,128)S(1)} %cholesky.543), custom_call_target="Cholesky" | custom-call | tf_op jit(solution)/shard_map/jit(cholesky)/cholesky | solution.py:109
  557.8 10.4 %custom-call.66 = f32[1,128,128]{1,2,0:T(8,128)} custom-call(f32[1,128,128]{2,1,0:T(8,128)S(1)} %get-tuple-element.34), custom_call_target="InvertDiagBlocksLowerTriangular" | custom-call | tf_op jit(solution)/shard_map/jit(cholesky)/cholesky | solution.py:109
  569.4 1.7 convolution_subtract_fusion.2
  571.1 11.9 %cholesky.451 = f32[128,128]{1,0:T(8,128)S(1)} custom-call(f32[128,128]{1,0:T(8,128)S(1)} %cholesky.548), custom_call_target="Cholesky" | custom-call | tf_op jit(solution)/shard_map/jit(cholesky)/cholesky | solution.py:109
  583.8 9.8 %custom-call.67 = f32[1,128,128]{1,2,0:T(8,128)S(1)} custom-call(f32[1,128,128]{2,1,0:T(8,128)S(1)} %get-tuple-element.31), custom_call_target="InvertDiagBlocksLowerTriangular" | custom-call | tf_op jit(solution)/shard_map/jit(cholesky)/cholesky | solution.py:109
  593.9 1.7 convolution_subtract_fusion.3
  595.6 11.7 %cholesky.470 = f32[128,128]{1,0:T(8,128)S(1)} custom-call(f32[128,128]{1,0:T(8,128)S(1)} %cholesky.553), custom_call_target="Cholesky" | custom-call | tf_op jit(solution)/shard_map/jit(cholesky)/cholesky | solution.py:109
  608.0 9.8 %custom-call.68 = f32[1,128,128]{1,2,0:T(8,128)S(1)} custom-call(f32[1,128,128]{2,1,0:T(8,128)S(1)} %get-tuple-element.28), custom_call_target="InvertDiagBlocksLowerTriangular" | custom-call | tf_op jit(solution)/shard_map/jit(cholesky)/cholesky | solution.py:109
  619.7 12.1 %cholesky.490 = f32[128,128]{1,0:T(8,128)S(1)} custom-call(f32[128,128]{1,0:T(8,128)S(1)} %cholesky.558), custom_call_target="Cholesky" | custom-call | tf_op jit(solution)/shard_map/jit(cholesky)/cholesky | solution.py:109
  632.4 9.8 %custom-call.69 = f32[1,128,128]{1,2,0:T(8,128)S(1)} custom-call(f32[1,128,128]{2,1,0:T(8,128)S(1)} %get-tuple-element.25), custom_call_target="InvertDiagBlocksLowerTriangular" | custom-call | tf_op jit(solution)/shard_map/jit(cholesky)/cholesky | solution.py:109
  643.6 8.8 %cholesky.511 = f32[96,96]{1,0:T(8,128)S(1)} custom-call(f32[96,96]{1,0:T(8,128)S(1)} %convolution_subtract_fusion.5), custom_call_target="Cholesky" | custom-call | tf_op jit(solution)/shard_map/jit(cholesky)/cholesky | solution.py:109
  660.3 18.0 %while.1 = (s32[]{:T(128)}, f32[864,864]{1,0:T(8,128)}, s32[6,2]{0,1:T(2,128)S(1)}, f32[6,128,128]{2,1,0:T(8,128)S(1)}, s32[]{:T(128)}) while((s32[]{:T(128)}, f32[864,864]{1,0:T(8,128)}, s32[6,2]{0,1:T(2,128)S(1)}, f32[6,128,128]{2,1,0:T(8,128)S(1)}, s32[]{:T(128)}) %tuple.58), condition=%wide.while_cond, body=%wide.while_body.sunk | while | flops 2 | bytes 131181 | solution.py:28
  661.0 2.3 bitcast_dynamic-update-slice_fusion.2
  664.0 2.3 bitcast_dynamic-update-slice_fusion.2
  667.0 2.3 bitcast_dynamic-update-slice_fusion.2
  670.0 2.3 bitcast_dynamic-update-slice_fusion.2
  673.0 2.3 bitcast_dynamic-update-slice_fusion.2
  676.0 2.3 bitcast_dynamic-update-slice_fusion.2
  680.2 69.7 %custom-call.70 = f32[7,128,128]{1,2,0:T(8,128)S(1)} custom-call(f32[7,128,128]{2,1,0:T(8,128)} %pad_maximum_fusion), custom_call_target="InvertDiagBlocksLowerTriangular" | custom-call | tf_op jit(solution)/shard_map/triangular_solve | solution.py:28
  754.0 4.2 cholesky.524
  759.7 2.0 fusion.102
  761.6 3.8 custom-call.71
  (199 shorter events, 76.2 us)
Async XLA Ops:
  7.2 468.4 %all-reduce.7.cloned.1.call-start = ((), (), s32[]{:S(2)}) async-start(), calls=%async_computation | async-start | bytes 6422528 | tf_op jit(solution)/shard_map/psum | solution.py:88
  9.1 49.7 %collective-permute-start = (bf16[1,32,1,128,128]{4,1,3,2,0:T(8,128)(2,1)S(1)}, bf16[1,32,1,128,128]{4,1,3,2,0:T(8,128)(2,1)S(1)}, u32[]{:S(2)}, u32[]{:S(2)}) collective-permute-start(bf16[1,32,1,128,128]{4,1,3,2,0:T(8,128)(2,1)S(1)} %copy.40), channel_id=1, source_target_pairs={{0,1},{1,2},{2,3},{3,4},{4,5},{5,6},{6,7},{8,9},{9,10},{10,11},{11... | collective-permute-start | bytes 3145736 | tf_op jit(solution)/shard_map/ppermute | solution.py:20
  14.1 44.8 %collective-permute-start.1 = (bf16[1,32,1,128,128]{4,1,3,2,0:T(8,128)(2,1)S(1)}, bf16[1,32,1,128,128]{4,1,3,2,0:T(8,128)(2,1)S(1)}, u32[]{:S(2)}, u32[]{:S(2)}) collective-permute-start(bf16[1,32,1,128,128]{4,1,3,2,0:T(8,128)(2,1)S(1)} %copy.40), channel_id=1, source_target_pairs={{1,0},{2,1},{3,2},{4,3},{5,4},{6,5},{7,6},{9,8},{10,9},{11,10},{12... | collective-permute-start | bytes 3145736 | tf_op jit(solution)/shard_map/ppermute | solution.py:21
  21.0 45.7 %copy-start.4 = (bf16[1,32,1,128,128]{4,3,2,1,0:T(8,128)(2,1)S(1)}, bf16[1,32,1,128,128]{4,3,2,1,0:T(8,128)(2,1)}, u32[]{:S(2)}) copy-start(bf16[1,32,1,128,128]{4,3,2,1,0:T(8,128)(2,1)} %param.5) | copy-start | bytes 3145732
  58.9 7.8 copy-start.6
  58.9 7.8 copy-start.8
  328.4 2.9 copy-start.5
  328.4 2.9 copy-start.7
  328.6 3.7 copy-start.9
  331.3 1.8 copy-start.14
  331.3 1.8 copy-start.15
  331.4 1.8 copy-start.16
  331.4 1.8 copy-start.17
  331.4 1.8 copy-start.18
  331.4 1.8 copy-start.19
  331.4 1.8 copy-start.20
  331.4 1.8 copy-start.21
  331.4 1.8 copy-start.22
  331.4 1.8 copy-start.23
  331.4 1.8 copy-start.24
  334.0 3.4 copy-start.25
  385.7 1.9 copy-start.13
  475.6 3.5 copy-start
  487.9 1.6 copy-start.3
  658.4 0.9 copy-start.26
  658.4 1.9 copy-start.12
  658.6 1.7 copy-start.1
  678.3 94.2 %copy-start.2 = (f32[864,864]{1,0:T(8,128)S(1)}, f32[864,864]{1,0:T(8,128)}, u32[]{:S(2)}) copy-start(f32[864,864]{1,0:T(8,128)} %get-tuple-element.120) | copy-start | bytes 8957956
  766.3 11.4 %copy-start.11 = (f32[32,864]{1,0:T(8,128)}, f32[32,864]{1,0:T(8,128)S(1)}, u32[]{:S(2)}) copy-start(f32[32,864]{1,0:T(8,128)S(1)} %broadcast_multiply_fusion) | copy-start | bytes 331780
  766.3 11.4 %copy-start.10 = (f32[32,864]{1,0:T(8,128)S(1)}, f32[32,864]{1,0:T(8,128)}, u32[]{:S(2)}) copy-start(f32[32,864]{1,0:T(8,128)} %get-tuple-element.18) | copy-start | bytes 331780
Sparse Core Ops, SparseCore 0:
  334.2 141.3 all-reduce.6
where the time goes:
time: 794 us; the launch traced here: 787 us
  local copies, waits for them, and re-layouts  276 us (35%)
  other arithmetic  255 us (32%)
  waiting for transfers between devices  126 us (16%)
  matrix products  59 us (7%)
  blocking collectives  41.9 us (5%)
  between operations  22 us (3%)
    gather x5, local copies, waits for them, and re-layouts, take_columns(): return jnp.take(matrix, indices, axis=1)  219 us
    another operation x26, other arithmetic, shards(): chol_acts = jnp.linalg.cholesky(damped_activation_factor)  149 us
    psum x1, waiting for transfers between devices, shards(): lax.psum((gram, gradient_gram_matrix, gradient_portion), ('dp', 'slab'))  88 us
    another operation x9, other arithmetic, cholesky_apply(): lax.linalg.triangular_solve(factor, halfway, left_side=True, lower=True,...  78.2 us
    psum x1, blocking collectives, shards(): lax.psum((gram, gradient_gram_matrix, gradient_portion), ('dp', 'slab'))  41.9 us
    ppermute x1, waiting for transfers between devices, padded_2(): before = lax.ppermute(last, axis, up)  37.8 us
    dot_general x27, matrix products, shards(): lax.dot_general(grad_rows, shifted, (((0, 2), (0, 2)), ((), ())), preferr...  31.2 us
    another operation x18, local copies, waits for them, and re-layouts  17.9 us
  transfers between devices with their start and end apart: 3, of which 2 were waited for; matrix products, arithmetic and copies ran while one was open for 2% of the time, Pallas kernels for 0%

commit v1 on v0

--- a/solution.py
+++ b/solution.py
@@ -86,7 +86,7 @@
         "mfuh,mioh->fuio", input_patches, input_patches, preferred_element_type=jnp.float32
     ).reshape(27 * channels, 27 * channels)
     summed_acts, summed_grads, summed_weight = lax.psum(
-        (gram, gradient_gram_matrix, gradient_portion), ("dp", "slab")
+        lax.psum((gram, gradient_gram_matrix, gradient_portion), "slab"), "dp"
     )
     positions = (
         volumes * lax.axis_size("dp") * planes * lax.axis_size("slab") * height * kernel_extent

time: 794 us -> 856 us (1.078)
  waiting for transfers between devices: 126 us -> 184 us
    psum x1 -> x2, waiting for transfers between devices: 88 us -> 147 us  [the longest x1 134 us: shards(): lax.psum((gram, gradient_gram_matrix, gradient_portion), 'slab')]
    psum x1 -> x2, blocking collectives: 41.9 us -> 46.6 us  [the longest x1 34.8 us: shards(): lax.psum((gram, gradient_gram_matrix, gradient_portion), 'slab')]
  transfers between devices with their start and end apart: 3 -> 4, of which waited for: 2 -> 3; matrix products, arithmetic and copies ran while one was open for 2% -> 2% of each run, Pallas kernels for 0% -> 0%
where the time goes in v1:
time: 856 us; the launch traced here: 849 us
  local copies, waits for them, and re-layouts  276 us (32%)
  other arithmetic  255 us (30%)
  waiting for transfers between devices  184 us (21%)
  matrix products  59 us (7%)
  blocking collectives  46.6 us (5%)
  between operations  21.9 us (3%)
    gather x5, local copies, waits for them, and re-layouts, take_columns(): return jnp.take(matrix, indices, axis=1)  219 us
    another operation x26, other arithmetic, shards(): chol_acts = jnp.linalg.cholesky(damped_activation_factor)  149 us
    psum x1, waiting for transfers between devices, shards(): lax.psum((gram, gradient_gram_matrix, gradient_portion), 'slab')  134 us
    another operation x9, other arithmetic, cholesky_apply(): lax.linalg.triangular_solve(factor, halfway, left_side=True, lower=True,...  78.2 us
    ppermute x1, waiting for transfers between devices, padded_2(): before = lax.ppermute(last, axis, up)  37.8 us
    psum x1, blocking collectives, shards(): lax.psum((gram, gradient_gram_matrix, gradient_portion), 'slab')  34.8 us
    dot_general x27, matrix products, shards(): lax.dot_general(grad_rows, shifted, (((0, 2), (0, 2)), ((), ())), preferr...  31.2 us
    another operation x18, local copies, waits for them, and re-layouts  17.4 us
  transfers between devices with their start and end apart: 4, of which 3 were waited for; matrix products, arithmetic and copies ran while one was open for 2% of the time, Pallas kernels for 0%

profile of v1, /device:TPU:0, one launch (start us, length us, event | category | flops | bytes accessed | tf_op | source)
XLA Modules:
  0.0 849.3 jit_solution(3382944170378576890)
XLA Ops:
  7.2 1.9 copy.40
  9.1 4.9 collective-permute-start
  18.2 2.8 convolution_bitcast_fusion.13
  21.0 37.8 %collective-permute-done = bf16[1,32,1,128,128]{4,1,3,2,0:T(8,128)(2,1)S(1)} collective-permute-done((bf16[1,32,1,128,128]{4,1,3,2,0:T(8,128)(2,1)S(1)}, bf16[1,32,1,128,128]{4,1,3,2,0:T(8,128)(2,1)S(1)}, u32[]{:S(2)}, u32[]{:S(2)}) %collective-permute-start) | collective-permute-done | bytes 1048608 | tf_op jit(solution)/shard_map/ppermute | solution.py:20
  58.9 7.8 select_maximum_fusion
  93.4 6.5 copy.71
  99.9 6.9 reshape.605
  106.8 8.9 %copy.72 = bf16[1,32,50700]{1,2,0:T(8,128)(2,1)} copy(bf16[1,32,50700]{2,1,0:T(8,128)(2,1)S(1)} %reshape.605) | data formatting | bytes 6489600 | tf_op jit(solution)/shard_map/reshape | solution.py:77
  115.7 209.4 %gather_fusion = bf16[13824,32]{1,0:T(8,128)(2,1)} fusion(bf16[1,32,50700]{1,2,0:T(8,128)(2,1)} %copy.72, s32[13824]{0:T(1024)S(1)} %fusion.81), kind=kCustom, calls=%fused_computation | custom fusion | bytes 1880064 | tf_op jit(solution)/shard_map/vmap(jit(_take))/gather | solution.py:34
  325.2 3.2 copy.73
  328.6 2.8 fusion.151
  334.1 133.5 %all-reduce.9.cloned.1.call-done = (f32[32,864]{1,0:T(8,128)}, f32[864,864]{1,0:T(8,128)}) async-done(((f32[32,864]{1,0:T(8,128)}, f32[864,864]{1,0:T(8,128)}), (f32[32,864]{1,0:T(8,128)}, f32[864,864]{1,0:T(8,128)})) %all-reduce.9.cloned.1.call-update) | async-done | bytes 3096592 | tf_op jit(solution)/shard_map/psum | solution.py:89
  467.6 3.3 copy.74
  471.0 6.1 gather_fusion.1
  477.5 34.8 %psum.46 = f32[32,32]{1,0:T(8,128)S(1)} all-reduce(f32[32,32]{1,0:T(8,128)S(1)} %fusion.34), channel_id=1, replica_groups=mesh['dp'=4,'slab'=8] {'slab'}, use_global_device_ids=true, to_apply=%region_5.6 | all-reduce | flops 1024 | bytes 8192 | tf_op jit(solution)/shard_map/psum | solution.py:89
  512.3 11.7 %psum.47 = f32[32,32]{1,0:T(8,128)S(1)} all-reduce(f32[32,32]{1,0:T(8,128)S(1)} %psum.46), channel_id=1, replica_groups=mesh['dp'=4,'slab'=8] {'dp'}, use_global_device_ids=true, to_apply=%region_6.7 | all-reduce | flops 1024 | bytes 8192 | tf_op jit(solution)/shard_map/psum | solution.py:88
  525.9 13.0 %all-reduce.11.cloned.1.call-done = (f32[32,864]{1,0:T(8,128)}, f32[864,864]{1,0:T(8,128)}) async-done(((f32[32,864]{1,0:T(8,128)}, f32[864,864]{1,0:T(8,128)}), (f32[32,864]{1,0:T(8,128)}, f32[864,864]{1,0:T(8,128)})) %all-reduce.11.cloned.1.call-update) | async-done | bytes 3096592 | tf_op jit(solution)/shard_map/psum | solution.py:88
  538.9 2.7 select_reduce_fusion
  542.4 1.9 select_add_fusion
  544.3 4.7 copy.75
  549.0 2.3 fusion.6
  551.2 1.6 copy-done.3
  552.9 11.7 %cholesky.204 = f32[128,128]{1,0:T(8,128)S(1)} custom-call(f32[128,128]{1,0:T(8,128)S(1)} %cholesky.534), custom_call_target="Cholesky" | custom-call | tf_op jit(solution)/shard_map/jit(cholesky)/cholesky | solution.py:109
  564.9 9.8 %custom-call.64 = f32[1,128,128]{1,2,0:T(8,128)S(1)} custom-call(f32[1,128,128]{2,1,0:T(8,128)S(1)} %get-tuple-element.42), custom_call_target="InvertDiagBlocksLowerTriangular" | custom-call | tf_op jit(solution)/shard_map/jit(cholesky)/cholesky | solution.py:109
  578.2 13.2 %cholesky.227 = f32[128,128]{1,0:T(8,128)} custom-call(f32[128,128]{1,0:T(8,128)} %cholesky.538), custom_call_target="Cholesky" | custom-call | tf_op jit(solution)/shard_map/jit(cholesky)/cholesky | solution.py:109
  592.9 11.4 %custom-call.65 = f32[1,128,128]{1,2,0:T(8,128)} custom-call(f32[1,128,128]{2,1,0:T(8,128)} %get-tuple-element.39), custom_call_target="InvertDiagBlocksLowerTriangular" | custom-call | tf_op jit(solution)/shard_map/jit(cholesky)/cholesky | solution.py:109
  607.2 12.3 %cholesky.432 = f32[128,128]{1,0:T(8,128)} custom-call(f32[128,128]{1,0:T(8,128)S(1)} %cholesky.543), custom_call_target="Cholesky" | custom-call | tf_op jit(solution)/shard_map/jit(cholesky)/cholesky | solution.py:109
  621.0 10.4 %custom-call.66 = f32[1,128,128]{1,2,0:T(8,128)} custom-call(f32[1,128,128]{2,1,0:T(8,128)S(1)} %get-tuple-element.36), custom_call_target="InvertDiagBlocksLowerTriangular" | custom-call | tf_op jit(solution)/shard_map/jit(cholesky)/cholesky | solution.py:109
  632.7 1.7 convolution_subtract_fusion.2
  634.4 11.9 %cholesky.451 = f32[128,128]{1,0:T(8,128)S(1)} custom-call(f32[128,128]{1,0:T(8,128)S(1)} %cholesky.548), custom_call_target="Cholesky" | custom-call | tf_op jit(solution)/shard_map/jit(cholesky)/cholesky | solution.py:109
  647.0 9.8 %custom-call.67 = f32[1,128,128]{1,2,0:T(8,128)S(1)} custom-call(f32[1,128,128]{2,1,0:T(8,128)S(1)} %get-tuple-element.33), custom_call_target="InvertDiagBlocksLowerTriangular" | custom-call | tf_op jit(solution)/shard_map/jit(cholesky)/cholesky | solution.py:109
  657.2 1.7 convolution_subtract_fusion.3
  658.8 11.7 %cholesky.470 = f32[128,128]{1,0:T(8,128)S(1)} custom-call(f32[128,128]{1,0:T(8,128)S(1)} %cholesky.553), custom_call_target="Cholesky" | custom-call | tf_op jit(solution)/shard_map/jit(cholesky)/cholesky | solution.py:109
  671.3 9.8 %custom-call.68 = f32[1,128,128]{1,2,0:T(8,128)S(1)} custom-call(f32[1,128,128]{2,1,0:T(8,128)S(1)} %get-tuple-element.30), custom_call_target="InvertDiagBlocksLowerTriangular" | custom-call | tf_op jit(solution)/shard_map/jit(cholesky)/cholesky | solution.py:109
  682.9 12.1 %cholesky.490 = f32[128,128]{1,0:T(8,128)S(1)} custom-call(f32[128,128]{1,0:T(8,128)S(1)} %cholesky.558), custom_call_target="Cholesky" | custom-call | tf_op jit(solution)/shard_map/jit(cholesky)/cholesky | solution.py:109
  695.7 9.8 %custom-call.69 = f32[1,128,128]{1,2,0:T(8,128)S(1)} custom-call(f32[1,128,128]{2,1,0:T(8,128)S(1)} %get-tuple-element.27), custom_call_target="InvertDiagBlocksLowerTriangular" | custom-call | tf_op jit(solution)/shard_map/jit(cholesky)/cholesky | solution.py:109
  706.9 8.8 %cholesky.511 = f32[96,96]{1,0:T(8,128)S(1)} custom-call(f32[96,96]{1,0:T(8,128)S(1)} %convolution_subtract_fusion.5), custom_call_target="Cholesky" | custom-call | tf_op jit(solution)/shard_map/jit(cholesky)/cholesky | solution.py:109
  723.4 17.5 %while.1 = (s32[]{:T(128)}, f32[864,864]{1,0:T(8,128)}, s32[6,2]{0,1:T(2,128)S(1)}, f32[6,128,128]{2,1,0:T(8,128)S(1)}, s32[]{:T(128)}) while((s32[]{:T(128)}, f32[864,864]{1,0:T(8,128)}, s32[6,2]{0,1:T(2,128)S(1)}, f32[6,128,128]{2,1,0:T(8,128)S(1)}, s32[]{:T(128)}) %tuple.61), condition=%wide.while_cond, body=%wide.while_body.sunk | while | flops 2 | bytes 131181 | solution.py:28
  724.0 2.3 bitcast_dynamic-update-slice_fusion.2
  726.9 2.3 bitcast_dynamic-update-slice_fusion.2
  729.8 2.3 bitcast_dynamic-update-slice_fusion.2
  732.7 2.3 bitcast_dynamic-update-slice_fusion.2
  735.6 2.3 bitcast_dynamic-update-slice_fusion.2
  738.5 2.3 bitcast_dynamic-update-slice_fusion.2
  742.7 69.7 %custom-call.70 = f32[7,128,128]{1,2,0:T(8,128)S(1)} custom-call(f32[7,128,128]{2,1,0:T(8,128)} %pad_maximum_fusion), custom_call_target="InvertDiagBlocksLowerTriangular" | custom-call | tf_op jit(solution)/shard_map/triangular_solve | solution.py:28
  816.5 4.2 cholesky.524
  822.2 2.0 fusion.102
  824.1 3.8 custom-call.71
  (203 shorter events, 79.1 us)
Async XLA Ops:
  7.2 460.4 %all-reduce.9.cloned.1.call-start = ((), (), s32[]{:S(2)}) async-start(), calls=%async_computation | async-start | bytes 6422528 | tf_op jit(solution)/shard_map/psum | solution.py:89
  9.1 49.7 %collective-permute-start = (bf16[1,32,1,128,128]{4,1,3,2,0:T(8,128)(2,1)S(1)}, bf16[1,32,1,128,128]{4,1,3,2,0:T(8,128)(2,1)S(1)}, u32[]{:S(2)}, u32[]{:S(2)}) collective-permute-start(bf16[1,32,1,128,128]{4,1,3,2,0:T(8,128)(2,1)S(1)} %copy.40), channel_id=1, source_target_pairs={{0,1},{1,2},{2,3},{3,4},{4,5},{5,6},{6,7},{8,9},{9,10},{10,11},{11... | collective-permute-start | bytes 3145736 | tf_op jit(solution)/shard_map/ppermute | solution.py:20
  14.1 44.8 %collective-permute-start.1 = (bf16[1,32,1,128,128]{4,1,3,2,0:T(8,128)(2,1)S(1)}, bf16[1,32,1,128,128]{4,1,3,2,0:T(8,128)(2,1)S(1)}, u32[]{:S(2)}, u32[]{:S(2)}) collective-permute-start(bf16[1,32,1,128,128]{4,1,3,2,0:T(8,128)(2,1)S(1)} %copy.40), channel_id=1, source_target_pairs={{1,0},{2,1},{3,2},{4,3},{5,4},{6,5},{7,6},{9,8},{10,9},{11,10},{12... | collective-permute-start | bytes 3145736 | tf_op jit(solution)/shard_map/ppermute | solution.py:21
  21.0 45.7 %copy-start.4 = (bf16[1,32,1,128,128]{4,3,2,1,0:T(8,128)(2,1)S(1)}, bf16[1,32,1,128,128]{4,3,2,1,0:T(8,128)(2,1)}, u32[]{:S(2)}) copy-start(bf16[1,32,1,128,128]{4,3,2,1,0:T(8,128)(2,1)} %param.5) | copy-start | bytes 3145732
  58.9 7.8 copy-start.6
  58.9 7.8 copy-start.8
  328.4 2.9 copy-start.5
  328.4 2.9 copy-start.7
  328.6 3.7 copy-start.9
  331.3 1.8 copy-start.14
  331.3 1.8 copy-start.15
  331.3 1.8 copy-start.16
  331.4 1.8 copy-start.17
  331.4 1.8 copy-start.18
  331.4 1.8 copy-start.19
  331.4 1.8 copy-start.20
  331.4 1.8 copy-start.21
  331.4 1.8 copy-start.22
  331.4 1.8 copy-start.23
  331.4 1.8 copy-start.24
  334.0 204.9 %all-reduce.11.cloned.1.call-start = ((), (), s32[]{:S(2)}) async-start(), calls=%async_computation.1 | async-start | bytes 6422528 | tf_op jit(solution)/shard_map/psum | solution.py:88
  467.6 3.4 copy-start.25
  524.0 1.9 copy-start.13
  538.9 3.5 copy-start
  551.2 1.6 copy-start.3
  721.4 0.9 copy-start.26
  721.4 1.9 copy-start.12
  721.7 1.7 copy-start.1
  740.8 94.2 %copy-start.2 = (f32[864,864]{1,0:T(8,128)S(1)}, f32[864,864]{1,0:T(8,128)}, u32[]{:S(2)}) copy-start(f32[864,864]{1,0:T(8,128)} %get-tuple-element.126) | copy-start | bytes 8957956
  828.8 11.4 %copy-start.11 = (f32[32,864]{1,0:T(8,128)}, f32[32,864]{1,0:T(8,128)S(1)}, u32[]{:S(2)}) copy-start(f32[32,864]{1,0:T(8,128)S(1)} %broadcast_multiply_fusion) | copy-start | bytes 331780
  828.8 11.4 %copy-start.10 = (f32[32,864]{1,0:T(8,128)S(1)}, f32[32,864]{1,0:T(8,128)}, u32[]{:S(2)}) copy-start(f32[32,864]{1,0:T(8,128)} %get-tuple-element.20) | copy-start | bytes 331780
Sparse Core Ops, SparseCore 0:
  334.1 133.4 all-reduce.8
  470.0 68.8 all-reduce.10
